TPU v7x, 32 devices: a whole 2x2x4 slice. The times are simulated.
32 devices in a mesh: graph: 8 (over y, x, core), rep: 4 (over z).
Axes of the slice: x: 2, y: 2, z: 4, core: 2. Of those that a mesh axis runs over, the one named last changes fastest.
Arguments:
- nodes: bfloat16 [4, 64, 32, 256], P('rep', 'graph'), may hold values from -20 to 20, as said below
- cotangent: bfloat16 [4, 64, 32, 256], P('rep', 'graph'), may hold values from -6 to 6
- live: int32 [4, 64], P('rep', 'graph'), may hold values from 2 to 32, as said below
- partner_first: int32 [4, 64], P('rep', 'graph'), may hold values from 0 to 63, as said below
- partner_size: int32 [4, 64], P('rep', 'graph'), may hold values from 1 to 2
- edge_src: int32 [4, 2048], P('rep', 'graph'), may hold values from 0 to 255, as said below
- edge_dst: int32 [4, 2048], P('rep', 'graph'), may hold values from 0 to 255, as said below
- w_edge1: bfloat16 [512, 512], replicated, may hold values from -0.25 to 0.25
- b_edge: float32 [512], replicated, may hold values from -3 to 3
- w_edge2: bfloat16 [512, 256], replicated, may hold values from -0.25 to 0.25
- w_node1: bfloat16 [768, 512], replicated, may hold values from -0.21875 to 0.21875
- b_node: float32 [512], replicated, may hold values from -3 to 3
- w_node2: bfloat16 [512, 256], replicated, may hold values from -0.25 to 0.25
Outputs:
- updated: bfloat16 [4, 64, 32, 256], P('rep', 'graph')
- d_nodes: bfloat16 [4, 64, 32, 256], P('rep', 'graph')
- g_edge1: float32 [512, 512], P('rep')
- g_bedge: float32 [512], P('rep')
- g_edge2: float32 [512, 256], P('rep')
- g_node1: float32 [768, 512], P('rep')
- g_bnode: float32 [512], P('rep')
- g_node2: float32 [512, 256], P('rep')
Inputs may be any that keep to these rules, and one draw needn't show every extreme that they name: A graph is one or two consecutive granules of one device, and every granule of a graph but its last is full; rows beyond live are padding. `partner_first`: index within the replica of the first granule of the partner graph, the same for all granules of a graph; pairing is mutual. Graphs in the lower half of a device's 8 granules pair with graphs in the upper half of some device's granules; the upper-half graphs of one device have partners on distinct devices. Within a replica every half of every device holds the same number of two-granule graphs. `edge_src`: row index within the device (granule times 32 plus row); both ends of an edge are live rows of the same graph. `edge_dst`: as edge_src. `nodes`: padding rows are zero.
All inputs are finite; a program needn't handle non-finite values.
Results may differ from a plain program's by a relative error of at most 0.023.
Values may be sent and summed in bfloat16 or wider, within the bound.
A program may use at most 128 MiB of HBM per device.

v0:
```python
import jax
import jax.numpy as jnp
from jax import lax
from jax.sharding import PartitionSpec as P

GMAX = 2


def silu_slope(values):
    sigmoid_value = jax.nn.sigmoid(values)
    return sigmoid_value * (1.0 + values * (1.0 - sigmoid_value))


def attend(queries, key_rows, key_mask):
    scale_factor = queries.shape[-1] ** (-0.5)
    scores = (
        jnp.einsum("gqh,gkh->gqk", queries, key_rows, preferred_element_type=jnp.float32)
        * scale_factor
    )
    scores = jnp.where(key_mask[:, None, :], scores, -jnp.inf)
    highest = jnp.max(scores, axis=-1, keepdims=True)
    powers = jnp.exp(scores - highest)
    softmax_out = powers / jnp.sum(powers, axis=-1, keepdims=True)
    softmax_low = softmax_out.astype(jnp.bfloat16)
    context = jnp.einsum("gqk,gkh->gqh", softmax_low, key_rows, preferred_element_type=jnp.float32)
    moved_rows = (queries.astype(jnp.float32) - context).astype(jnp.bfloat16)
    return (moved_rows, softmax_out, softmax_low)


def attend_back(queries, key_rows, softmax_out, softmax_low, grad_moved):
    scale_factor = queries.shape[-1] ** (-0.5)
    negated = -grad_moved
    grad_probs = jnp.einsum("gqh,gkh->gqk", negated, key_rows, preferred_element_type=jnp.float32)
    grad_keys = jnp.einsum("gqk,gqh->gkh", softmax_low, negated, preferred_element_type=jnp.float32)
    inner_sum = jnp.sum(softmax_out * grad_probs, axis=-1, keepdims=True)
    grad_scores = (softmax_out * (grad_probs - inner_sum) * scale_factor).astype(jnp.bfloat16)
    grad_queries = jnp.einsum(
        "gqk,gkh->gqh", grad_scores, key_rows, preferred_element_type=jnp.float32
    ) + grad_moved.astype(jnp.float32)
    grad_keys = grad_keys + jnp.einsum(
        "gqk,gqh->gkh", grad_scores, queries, preferred_element_type=jnp.float32
    )
    return (grad_queries, grad_keys)


def message_forward(node_rows, w_edge1, b_edge, w_edge2, sources, targets):
    state_width = node_rows.shape[1]
    pre_target = (
        jnp.dot(node_rows, w_edge1[:state_width], preferred_element_type=jnp.float32) + b_edge
    ).astype(jnp.bfloat16)
    pre_source = jnp.dot(
        node_rows, w_edge1[state_width:], preferred_element_type=jnp.float32
    ).astype(jnp.bfloat16)
    summed = pre_target[targets].astype(jnp.float32) + pre_source[sources].astype(jnp.float32)
    gathered = jax.ops.segment_sum(
        jax.nn.silu(summed), targets, num_segments=node_rows.shape[0]
    ).astype(jnp.bfloat16)
    message = jnp.dot(gathered, w_edge2, preferred_element_type=jnp.float32).astype(jnp.bfloat16)
    return (message, gathered, summed)


def message_backward(node_rows, w_edge1, w_edge2, sources, targets, gathered, summed, grad_message):
    state_width = node_rows.shape[1]
    grad_w2 = jnp.einsum("rf,rh->fh", gathered, grad_message, preferred_element_type=jnp.float32)
    grad_gathered = jnp.einsum(
        "rh,fh->rf", grad_message, w_edge2, preferred_element_type=jnp.float32
    ).astype(jnp.bfloat16)
    edge_grad = grad_gathered[targets].astype(jnp.float32) * silu_slope(summed)
    grad_target = jax.ops.segment_sum(edge_grad, targets, num_segments=node_rows.shape[0]).astype(
        jnp.bfloat16
    )
    grad_source = jax.ops.segment_sum(edge_grad, sources, num_segments=node_rows.shape[0]).astype(
        jnp.bfloat16
    )
    grad_w1 = jnp.concatenate(
        [
            jnp.einsum("rh,rf->hf", node_rows, grad_target, preferred_element_type=jnp.float32),
            jnp.einsum("rh,rf->hf", node_rows, grad_source, preferred_element_type=jnp.float32),
        ],
        axis=0,
    )
    grad_bias = jnp.sum(grad_target.astype(jnp.float32), axis=0)
    grad_rows = jnp.einsum(
        "rf,hf->rh", grad_target, w_edge1[:state_width], preferred_element_type=jnp.float32
    ) + jnp.einsum(
        "rf,hf->rh", grad_source, w_edge1[state_width:], preferred_element_type=jnp.float32
    )
    return (grad_rows, grad_w1, grad_bias, grad_w2)


def update_forward(node_rows, message, moved_flat, w_node1, b_node, w_node2, row_mask):
    state_width = node_rows.shape[1]
    hidden_pre = (
        jnp.dot(node_rows, w_node1[:state_width], preferred_element_type=jnp.float32)
        + jnp.dot(
            message, w_node1[state_width : 2 * state_width], preferred_element_type=jnp.float32
        )
        + jnp.dot(moved_flat, w_node1[2 * state_width :], preferred_element_type=jnp.float32)
        + b_node
    )
    active = jax.nn.silu(hidden_pre).astype(jnp.bfloat16)
    updated = jnp.where(
        row_mask,
        node_rows.astype(jnp.float32)
        + jnp.dot(active, w_node2, preferred_element_type=jnp.float32),
        0.0,
    ).astype(jnp.bfloat16)
    return (updated, hidden_pre, active)


def update_backward(node_rows, message, moved_flat, w_node1, w_node2, hidden_pre, active, grad_out):
    state_width = node_rows.shape[1]
    grad_w2 = jnp.einsum("rf,rh->fh", active, grad_out, preferred_element_type=jnp.float32)
    grad_hidden = (
        jnp.einsum("rh,fh->rf", grad_out, w_node2, preferred_element_type=jnp.float32)
        * silu_slope(hidden_pre)
    ).astype(jnp.bfloat16)
    grad_w1 = jnp.concatenate(
        [
            jnp.einsum("rh,rf->hf", node_rows, grad_hidden, preferred_element_type=jnp.float32),
            jnp.einsum("rh,rf->hf", message, grad_hidden, preferred_element_type=jnp.float32),
            jnp.einsum("rh,rf->hf", moved_flat, grad_hidden, preferred_element_type=jnp.float32),
        ],
        axis=0,
    )
    grad_bias = jnp.sum(grad_hidden.astype(jnp.float32), axis=0)
    grad_rows = grad_out.astype(jnp.float32) + jnp.einsum(
        "rf,hf->rh", grad_hidden, w_node1[:state_width], preferred_element_type=jnp.float32
    )
    grad_message = jnp.einsum(
        "rf,hf->rh",
        grad_hidden,
        w_node1[state_width : 2 * state_width],
        preferred_element_type=jnp.float32,
    ).astype(jnp.bfloat16)
    grad_moved = jnp.einsum(
        "rf,hf->rh", grad_hidden, w_node1[2 * state_width :], preferred_element_type=jnp.float32
    ).astype(jnp.bfloat16)
    return (grad_rows, grad_message, grad_moved, grad_w1, grad_bias, grad_w2)


def on_device(
    nodes,
    cotangent,
    live,
    partner_first,
    partner_size,
    edge_src,
    edge_dst,
    w_edge1,
    b_edge,
    w_edge2,
    w_node1,
    b_node,
    w_node2,
):
    local_nodes = nodes[0]
    granules, block_rows, state_width = local_nodes.shape
    half_count = granules // 2
    peer_count = lax.axis_size("graph")
    live_counts = live[0]
    partners = partner_first[0]
    partner_device = partners // granules
    same_before = jnp.concatenate([jnp.zeros((1,), jnp.bool_), partners[1:] == partners[:-1]])
    place_index = same_before.astype(jnp.int32)
    positions = jnp.arange(block_rows, dtype=jnp.int32)
    spans = jnp.arange(GMAX, dtype=jnp.int32)
    row_mask = (positions[None, :] < live_counts[:, None]).reshape(-1, 1)
    node_rows = local_nodes.reshape(-1, state_width)
    sources = edge_src[0]
    targets = edge_dst[0]
    slot_count = peer_count * 2 * GMAX
    send_offset = jnp.where(jnp.arange(granules, dtype=jnp.int32) < half_count, GMAX, 0)
    send_slot = partner_device * (2 * GMAX) + send_offset + place_index
    outgoing = (
        jnp.zeros((slot_count, block_rows, state_width), jnp.bfloat16)
        .at[send_slot]
        .set(local_nodes)
    )
    lives_out = jnp.zeros((slot_count,), jnp.int32).at[send_slot].set(live_counts)
    arrived, arrived_lives = (
        lax.all_to_all(outgoing, "graph", split_axis=0, concat_axis=0, tiled=True),
        lax.all_to_all(lives_out, "graph", split_axis=0, concat_axis=0, tiled=True),
    )
    message, gathered, summed = message_forward(
        node_rows, w_edge1, b_edge, w_edge2, sources, targets
    )
    read_slot = (
        partner_device[:, None] * (2 * GMAX) + (GMAX - send_offset)[:, None] + spans[None, :]
    )
    keys_all = arrived[read_slot].reshape(granules, GMAX * block_rows, state_width)
    mask_all = (positions[None, None, :] < arrived_lives[read_slot][:, :, None]).reshape(
        granules, GMAX * block_rows
    )
    moved_rows, probs_all, low_all = attend(local_nodes, keys_all, mask_all)
    moved_flat = moved_rows.reshape(-1, state_width)
    updated, hidden_pre, active = update_forward(
        node_rows, message, moved_flat, w_node1, b_node, w_node2, row_mask
    )
    grad_out = jnp.where(
        row_mask, cotangent[0].reshape(-1, state_width), jnp.zeros((), jnp.bfloat16)
    )
    grad_rows, grad_message, grad_moved, grad_n1, grad_bn, grad_n2 = update_backward(
        node_rows, message, moved_flat, w_node1, w_node2, hidden_pre, active, grad_out
    )
    grad_moved_blocks = grad_moved.reshape(granules, block_rows, state_width)
    query_all, key_all = attend_back(local_nodes, keys_all, probs_all, low_all, grad_moved_blocks)
    slot_grad = (
        jnp.zeros((slot_count, block_rows, state_width), jnp.float32)
        .at[read_slot.reshape(-1)]
        .add(key_all.reshape(granules * GMAX, block_rows, state_width))
    )
    back_grad = lax.all_to_all(
        slot_grad.astype(jnp.bfloat16), "graph", split_axis=0, concat_axis=0, tiled=True
    ).astype(slot_grad.dtype)
    attention_grad = query_all + back_grad[send_slot]
    message_rows, grad_e1, grad_be, grad_e2 = message_backward(
        node_rows, w_edge1, w_edge2, sources, targets, gathered, summed, grad_message
    )
    total_grad = grad_rows + attention_grad.reshape(-1, state_width) + message_rows
    d_nodes = jnp.where(row_mask, total_grad, 0.0).astype(jnp.bfloat16)
    partial_grads = (grad_e1, grad_be, grad_e2, grad_n1, grad_bn, grad_n2)
    summed_all = lax.psum(
        (
            partial_grads[0],
            partial_grads[1],
            partial_grads[2],
            partial_grads[3],
            partial_grads[4],
            partial_grads[5],
        ),
        ("graph", "rep"),
    )
    replica_index = lax.axis_index("rep")
    replica_count = lax.axis_size("rep")
    shares = tuple(
        (
            lax.dynamic_slice_in_dim(
                summed_grad,
                replica_index * (summed_grad.shape[0] // replica_count),
                summed_grad.shape[0] // replica_count,
                0,
            )
            for summed_grad in summed_all
        )
    )
    scale_factor = (lax.axis_size("graph") * lax.axis_size("rep") * granules * block_rows) ** (-0.5)
    scaled = tuple((summed_grad * scale_factor for summed_grad in shares))
    return (
        updated.reshape(1, granules, block_rows, state_width),
        d_nodes.reshape(1, granules, block_rows, state_width),
        scaled[0],
        scaled[1],
        scaled[2],
        scaled[3],
        scaled[4],
        scaled[5],
    )


def solution(mesh):
    placed = (
        P("rep", "graph", None, None),
        P("rep", "graph", None, None),
        P("rep", "graph"),
        P("rep", "graph"),
        P("rep", "graph"),
        P("rep", "graph"),
        P("rep", "graph"),
        P(),
        P(),
        P(),
        P(),
        P(),
        P(),
    )
    return jax.shard_map(
        on_device,
        mesh=mesh,
        in_specs=placed,
        out_specs=(
            P("rep", "graph", None, None),
            P("rep", "graph", None, None),
            P("rep", None),
            P("rep"),
            P("rep", None),
            P("rep", None),
            P("rep"),
            P("rep", None),
        ),
        check_vma=False,
    )
```

profile of v0, /device:TPU:0, one launch (start us, length us, event | category | flops | bytes accessed | tf_op | source)
XLA Modules:
  0.0 223.0 jit_solution(15581898955150633358)
XLA Ops:
  10.2 5.2 %all-to-all-start = ((s32[8,4,1]{1,2,0:T(1,128)}), s32[8,4,1]{1,2,0:T(1,128)S(1)}, u32[]{:S(2)}, u32[]{:S(2)}) async-start(s32[8,4,1]{1,2,0:T(1,128)} %bitcast.11), calls=%async_computation | async-start | bytes 8192 | tf_op jit(solution)/shard_map/all_to_all | solution.py:183
  17.0 1.2 fusion.43
  18.2 1.2 convolution_convert_fusion.1
  22.8 2.4 %scatter_custom_fusion = f32[256,512]{1,0:T(8,128)S(1)} fusion(s32[256]{0:T(256)S(1)} %bitcast.123, bf16[256,512]{1,0:T(8,128)(2,1)S(1)} %gather_fusion.1, bf16[256,512]{1,0:T(8,128)(2,1)S(1)} %gather_fusion, f32[]{:T(128)} %constant.24.clone.1, f32[]{:T(128)} %constant.21.clone.1), kind=kCustom, calls=%fused_computation.59 | custom fusion | flops 1048576 | bytes 1048584 | tf_op jit(solution)/shard_map/scatter-add | solution.py:55
  27.3 2.1 scatter_fusion
  29.4 4.2 %all-to-all-start.1 = ((bf16[32,32,256]{2,1,0:T(8,128)(2,1)}), bf16[32,32,256]{2,1,0:T(8,128)(2,1)}, u32[]{:S(2)}, u32[]{:S(2)}) async-start(bf16[32,32,256]{2,1,0:T(8,128)(2,1)} %scatter_fusion), calls=%async_computation.1 | async-start | bytes 1048576 | tf_op jit(solution)/shard_map/all_to_all | solution.py:182
  36.2 7.2 %all-to-all-done.1 = bf16[32,32,256]{2,1,0:T(8,128)(2,1)} async-done(((bf16[32,32,256]{2,1,0:T(8,128)(2,1)}), bf16[32,32,256]{2,1,0:T(8,128)(2,1)}, u32[]{:S(2)}, u32[]{:S(2)}) %all-to-all-start.1) | async-done | bytes 524320 | tf_op jit(solution)/shard_map/all_to_all | solution.py:182
  43.4 1.6 gather_fusion.3
  49.2 1.7 fusion.52
  59.8 2.6 %scatter_custom_fusion.4 = f32[256,512]{1,0:T(8,128)S(1)} fusion(s32[256]{0:T(256)} %bitcast.122, f32[]{:T(128)} %constant.21.clone.1, bf16[256,512]{1,0:T(8,128)(2,1)S(1)} %gather_fusion.5, bf16[256,512]{1,0:T(8,128)(2,1)S(1)} %gather_fusion.1, bf16[256,512]{1,0:T(8,128)(2,1)S(1)} %gather_fusion), kind=kCustom, calls=%fused_computation.68 | custom fusion | flops 1703936 | bytes 1311232 | tf_op jit(solution)/shard_map/scatter-add | solution.py:69
  62.4 2.8 %scatter_custom_fusion.5 = f32[256,512]{1,0:T(8,128)S(1)} fusion(s32[256]{0:T(256)} %bitcast.124, f32[]{:T(128)} %constant.21.clone.1, bf16[256,512]{1,0:T(8,128)(2,1)S(1)} %gather_fusion.5, bf16[256,512]{1,0:T(8,128)(2,1)S(1)} %gather_fusion.1, bf16[256,512]{1,0:T(8,128)(2,1)S(1)} %gather_fusion), kind=kCustom, calls=%fused_computation.66 | custom fusion | flops 1703936 | bytes 1311232 | tf_op jit(solution)/shard_map/scatter-add | solution.py:72
  67.0 1.3 pad_maximum_fusion
  68.4 2.3 %convolution_add_fusion = f32[8,64,256]{2,1,0:T(8,128)S(1)} fusion(f32[8,64,256]{2,1,0:T(8,128)S(1)} %fusion.52, f32[8,32,64]{2,1,0:T(8,128)} %fusion.74, bf16[1,8,32,256]{3,2,1,0:T(8,128)(2,1)S(1)} %copy-done.1, f32[8,32,64]{2,1,0:T(8,128)} %get-tuple-element.15, f32[8,32]{1,0:T(8,128)S(1)} %get-tuple-element.14), kind=kOutput, calls=%fused_computation.18 | convolution fusion | flops 8634687 | bytes 1311744 | tf_op jit(solution)/shard_map/gqk,gqh->gkh/dot_general | solution.py:40
  70.8 1.3 scatter_fusion.1
  73.1 3.6 %all-to-all-start.2 = ((bf16[32,32,256]{2,1,0:T(8,128)(2,1)}), bf16[32,32,256]{2,1,0:T(8,128)(2,1)S(1)}, u32[]{:S(2)}, u32[]{:S(2)}) async-start(bf16[32,32,256]{2,1,0:T(8,128)(2,1)} %convert_element_type.113), calls=%async_computation.2 | async-start | bytes 1048576 | tf_op jit(solution)/shard_map/all_to_all | solution.py:213
  76.8 46.2 %all-reduce = (f32[512]{0:T(512)S(1)}, f32[512]{0:T(512)S(1)}) all-reduce(f32[512]{0:T(512)S(1)} %convert_reduce_fusion.1, f32[512]{0:T(512)S(1)} %get-tuple-element.18), channel_id=1, replica_groups=mesh['graph'=8,'rep'=4] {'graph','rep'}, use_global_device_ids=true, to_apply=%region_11.12 | all-reduce | flops 1024 | bytes 8192 | tf_op jit(solution)/shard_map/psum | solution.py:223
  124.4 2.0 fusion.11
  127.6 1.8 gather_fusion.4
  129.4 2.2 fusion.6
  133.7 75.9 %all-reduce.4.cloned.1.call-done = (f32[512,512]{1,0:T(8,128)}, f32[512,256]{1,0:T(8,128)}, f32[768,512]{1,0:T(8,128)}, f32[512,256]{1,0:T(8,128)}) async-done(((f32[512,512]{1,0:T(8,128)}, f32[512,256]{1,0:T(8,128)}, f32[768,512]{1,0:T(8,128)}, f32[512,256]{1,0:T(8,128)}), (f32[512,512]{1,0:T(8,128)}, f32[512,256]{1,0:T(8,128)}, f32[768,512]{1,0:T(8,128)}, ...) | async-done | bytes 3670032 | tf_op jit(solution)/shard_map/psum | solution.py:223
  209.6 1.7 dynamic-slice_multiply_fusion.1
  211.3 1.6 dynamic-slice_multiply_fusion.3
  212.8 1.6 dynamic-slice_multiply_fusion.2
  214.4 1.8 dynamic-slice_multiply_fusion
  (119 shorter events, 33.1 us)
Async XLA Ops:
  7.2 40.3 %copy-start = (bf16[512,256]{1,0:T(8,128)(2,1)S(1)}, bf16[512,256]{1,0:T(8,128)(2,1)}, u32[]{:S(2)}) copy-start(bf16[512,256]{1,0:T(8,128)(2,1)} %param.24) | copy-start | bytes 786436
  7.2 12.3 %copy-start.1 = (bf16[1,8,32,256]{3,2,1,0:T(8,128)(2,1)S(1)}, bf16[1,8,32,256]{3,2,1,0:T(8,128)(2,1)}, u32[]{:S(2)}) copy-start(bf16[1,8,32,256]{3,2,1,0:T(8,128)(2,1)} %param.13) | copy-start | bytes 393220
  7.2 12.3 %copy-start.6 = (bf16[512,512]{1,0:T(8,128)(2,1)S(1)}, bf16[512,512]{1,0:T(8,128)(2,1)}, u32[]{:S(2)}) copy-start(bf16[512,512]{1,0:T(8,128)(2,1)} %param.19) | copy-start | bytes 1572868
  7.2 12.2 %copy-start.24 = (s32[1,256]{1,0:T(1,128)S(1)}, s32[1,256]{1,0:T(1,128)}, u32[]{:S(2)}) copy-start(s32[1,256]{1,0:T(1,128)} %param.18) | copy-start | bytes 3076
  7.2 12.2 %copy-start.25 = (s32[1,256]{1,0:T(1,128)S(1)}, s32[1,256]{1,0:T(1,128)}, u32[]{:S(2)}) copy-start(s32[1,256]{1,0:T(1,128)} %param.17) | copy-start | bytes 3076
  7.2 12.3 %copy-start.20 = (f32[512]{0:T(512)S(1)}, f32[512]{0:T(512)}, u32[]{:S(2)}) copy-start(f32[512]{0:T(512)} %param.20) | copy-start | bytes 6148
  10.2 19.2 %all-to-all-start = ((s32[8,4,1]{1,2,0:T(1,128)}), s32[8,4,1]{1,2,0:T(1,128)S(1)}, u32[]{:S(2)}, u32[]{:S(2)}) async-start(s32[8,4,1]{1,2,0:T(1,128)} %bitcast.11), calls=%async_computation | async-start | bytes 8192 | tf_op jit(solution)/shard_map/all_to_all | solution.py:183
  21.6 3.6 %copy-start.9 = (bf16[512,256]{1,0:T(8,128)(2,1)S(1)}, bf16[512,256]{1,0:T(8,128)(2,1)}, u32[]{:S(2)}) copy-start(bf16[512,256]{1,0:T(8,128)(2,1)} %param.21) | copy-start | bytes 786436
  22.8 2.6 %copy-start.2 = (bf16[768,512]{1,0:T(8,128)(2,1)S(1)}, bf16[768,512]{1,0:T(8,128)(2,1)}, u32[]{:S(2)}) copy-start(bf16[768,512]{1,0:T(8,128)(2,1)} %param.22) | copy-start | bytes 2359300
  25.4 8.4 %copy-start.18 = (bf16[1,8,32,256]{3,2,1,0:T(8,128)(2,1)S(1)}, bf16[1,8,32,256]{3,2,1,0:T(8,128)(2,1)}, u32[]{:S(2)}) copy-start(bf16[1,8,32,256]{3,2,1,0:T(8,128)(2,1)} %param.14) | copy-start | bytes 393220
  29.4 14.0 %all-to-all-start.1 = ((bf16[32,32,256]{2,1,0:T(8,128)(2,1)}), bf16[32,32,256]{2,1,0:T(8,128)(2,1)}, u32[]{:S(2)}, u32[]{:S(2)}) async-start(bf16[32,32,256]{2,1,0:T(8,128)(2,1)} %scatter_fusion), calls=%async_computation.1 | async-start | bytes 1048576 | tf_op jit(solution)/shard_map/all_to_all | solution.py:182
  33.6 176.0 %all-reduce.4.cloned.1.call-start = ((), (), s32[]{:S(2)}) async-start(), calls=%async_computation.3 | async-start | bytes 7340032 | tf_op jit(solution)/shard_map/psum | solution.py:223
  34.0 13.5 %copy-start.11 = (bf16[256,256]{1,0:T(8,128)(2,1)}, bf16[256,256]{1,0:T(8,128)(2,1)S(1)}, u32[]{:S(2)}) copy-start(bf16[256,256]{1,0:T(8,128)(2,1)S(1)} %bitcast_select_fusion) | copy-start | bytes 393220
  35.9 11.3 %copy-start.8 = (f32[256,512]{1,0:T(8,128)S(1)}, f32[256,512]{1,0:T(8,128)}, u32[]{:S(2)}) copy-start(f32[256,512]{1,0:T(8,128)} %convolution_add_fusion.2) | copy-start | bytes 1572868
  35.9 11.3 %copy-start.21 = (f32[512]{0:T(512)S(1)}, f32[512]{0:T(512)}, u32[]{:S(2)}) copy-start(f32[512]{0:T(512)} %param.23) | copy-start | bytes 6148
  50.8 3.4 %copy-start.17 = (bf16[8,32,256]{2,1,0:T(8,128)(2,1)S(1)}, bf16[8,32,256]{2,1,0:T(8,128)(2,1)}, u32[]{:S(2)}) copy-start(bf16[8,32,256]{2,1,0:T(8,128)(2,1)} %copy-done.16) | copy-start | bytes 393220
  54.3 3.2 %copy-start.12 = (bf16[256,256]{1,0:T(8,128)(2,1)S(1)}, bf16[256,256]{1,0:T(8,128)(2,1)}, u32[]{:S(2)}) copy-start(bf16[256,256]{1,0:T(8,128)(2,1)} %copy-done.11) | copy-start | bytes 393220
  54.3 3.2 %copy-start.15 = (f32[256,512]{1,0:T(8,128)S(1)}, f32[256,512]{1,0:T(8,128)}, u32[]{:S(2)}) copy-start(f32[256,512]{1,0:T(8,128)} %copy-done.14) | copy-start | bytes 1572868
  68.3 2.5 %copy-start.26 = (s32[16]{0:T(128)S(1)}, s32[16]{0:T(128)}, u32[]{:S(2)}) copy-start(s32[16]{0:T(128)} %fusion.60) | copy-start | bytes 196
  73.1 51.1 %copy-start.7 = (bf16[512,512]{1,0:T(8,128)(2,1)S(1)}, bf16[512,512]{1,0:T(8,128)(2,1)}, u32[]{:S(2)}) copy-start(bf16[512,512]{1,0:T(8,128)(2,1)} %param.19) | copy-start | bytes 1572868
  73.1 51.4 %copy-start.23 = (pred[256]{0:T(512)(128)(4,1)S(1)}, pred[256]{0:T(512)(128)(4,1)}, u32[]{:S(2)}) copy-start(pred[256]{0:T(512)(128)(4,1)} %copy-done.22) | copy-start | bytes 772
  73.1 53.4 %all-to-all-start.2 = ((bf16[32,32,256]{2,1,0:T(8,128)(2,1)}), bf16[32,32,256]{2,1,0:T(8,128)(2,1)S(1)}, u32[]{:S(2)}, u32[]{:S(2)}) async-start(bf16[32,32,256]{2,1,0:T(8,128)(2,1)} %convert_element_type.113), calls=%async_computation.2 | async-start | bytes 1048576 | tf_op jit(solution)/shard_map/all_to_all | solution.py:213
  126.4 2.9 %copy-start.19 = (bf16[256,256]{1,0:T(8,128)(2,1)S(1)}, bf16[256,256]{1,0:T(8,128)(2,1)}, u32[]{:S(2)}) copy-start(bf16[256,256]{1,0:T(8,128)(2,1)} %get-tuple-element.17) | copy-start | bytes 393220
  126.4 5.1 %copy-start.13 = (bf16[256,256]{1,0:T(8,128)(2,1)S(1)}, bf16[256,256]{1,0:T(8,128)(2,1)}, u32[]{:S(2)}) copy-start(bf16[256,256]{1,0:T(8,128)(2,1)} %copy-done.11) | copy-start | bytes 393220
  (7 other events, 9.2 us)
Sparse Core Ops, SparseCore 0:
  68.5 141.0 all-reduce.3
where the time goes:
time: 224 us; the launch traced here: 223 us
  waiting for transfers between devices  83.1 us (37%)
  blocking collectives  46.2 us (21%)
  other arithmetic  26.5 us (12%)
  matrix products  25 us (11%)
  local copies, waits for them, and re-layouts  14.6 us (7%)
  between operations  14.6 us (7%)
  starting transfers between devices  13.1 us (6%)
    psum x1, waiting for transfers between devices, on_device(): lax.psum((partial_grads[0], partial_grads[1], partial_grads[2], partial_g...  75.9 us
    psum x1, blocking collectives, on_device(): lax.psum((partial_grads[0], partial_grads[1], partial_grads[2], partial_g...  46.2 us
    mul x6, other arithmetic, on_device(): scaled = tuple((summed_grad * scale_factor for summed_grad in shares))  7.76 us
    all_to_all x1, waiting for transfers between devices, on_device(): lax.all_to_all(outgoing, 'graph', split_axis=0, concat_axis=0, tiled=True)  7.23 us
    all_to_all x1, starting transfers between devices, on_device(): lax.all_to_all(lives_out, 'graph', split_axis=0, concat_axis=0, tiled=True)  5.2 us
  transfers between devices with their start and end apart: 4, of which 2 were waited for; matrix products, arithmetic and copies ran while one was open for 14% of the time, Pallas kernels for 0%

commit v1 on v0

v1 whole, which is shorter than its diff:
```python
import functools

import jax
import jax.numpy as jnp
from jax import lax
from jax.experimental import pallas as pl
from jax.experimental.pallas import tpu as pltpu
from jax.sharding import PartitionSpec as P

GMAX = 2
LANES = 128
F32 = jnp.float32
BF16 = jnp.bfloat16


def dot_nn(a, b):
    return lax.dot_general(a, b, (((1,), (0,)), ((), ())), preferred_element_type=F32)


def dot_nt(a, b):
    return lax.dot_general(a, b, (((1,), (1,)), ((), ())), preferred_element_type=F32)


def dot_tn(a, b):
    return lax.dot_general(a, b, (((0,), (0,)), ((), ())), preferred_element_type=F32)


def sigmoid(v):
    return 1.0 / (1.0 + jnp.exp(-v))


def silu_slope(v, s):
    return s * (1.0 + v * (1.0 - s))


def round_up(value, unit):
    return -(-value // unit) * unit


def send(src, dst, send_sem, recv_sem, graph, rep):
    return pltpu.make_async_remote_copy(
        src_ref=src,
        dst_ref=dst,
        send_sem=send_sem,
        recv_sem=recv_sem,
        device_id={"graph": graph, "rep": rep},
        device_id_type=pl.DeviceIdType.MESH,
    )


class Reduce:
    def __init__(self, n_graph, n_rep, me, rep, refs):
        self.n, self.r, self.me, self.rep = n_graph, n_rep, me, rep
        (self.full, self.r0, self.a, self.r1, self.b, self.r2, self.got,
         self.s0, self.s1, self.v1, self.s2, self.v2, self.s3, self.v3) = refs
        self.chips = n_graph // 2
        self.core = lax.rem(me, 2)
        self.chip = lax.div(me, 2)
        self.half = self.full.shape[1] // 2
        self.ch = self.full.shape[1] // n_graph
        self.sends = []

    def go(self, copy):
        copy.start()
        self.sends.append(copy)

    def rows(self, start, size):
        return pl.ds(pl.multiple_of(start, 16), size)

    def start_core(self):
        other = 1 - self.core
        self.c0 = send(self.full.at[:, self.rows(other * self.half, self.half), :], self.r0,
                       self.s0.at[0], self.s0.at[1], self.chip * 2 + other, self.rep)
        self.go(self.c0)

    def start_plane(self):
        self.c0.wait_recv()
        mine = self.full[:, self.rows(self.core * self.half, self.half), :].astype(F32)
        self.a[...] = (mine + self.r0[...].astype(F32)).astype(BF16)
        self.c1 = []
        for d in range(1, self.chips):
            q = lax.rem(self.chip + d, self.chips)
            copy = send(self.a.at[:, self.rows(q * self.ch, self.ch), :], self.r1.at[d],
                        self.s1.at[d], self.v1.at[d], q * 2 + self.core, self.rep)
            self.go(copy)
            self.c1.append(copy)

    def start_rep(self):
        total = self.a[:, self.rows(self.chip * self.ch, self.ch), :].astype(F32)
        for copy in self.c1:
            copy.wait_recv()
        for d in range(1, self.chips):
            total = total + self.r1[d].astype(F32)
        self.b[...] = total.astype(BF16)
        self.c2 = []
        for d in range(1, self.r):
            z = lax.rem(self.rep + d, self.r)
            copy = send(self.b.at[z], self.r2.at[d], self.s2.at[d], self.v2.at[d], self.me, z)
            self.go(copy)
            self.c2.append(copy)

    def start_gather(self):
        total = self.b[self.rep].astype(F32)
        for copy in self.c2:
            copy.wait_recv()
        for d in range(1, self.r):
            total = total + self.r2[d].astype(F32)
        place = self.core * self.chips + self.chip
        self.got[place] = total.astype(BF16)
        self.c3 = []
        for d in range(1, self.n):
            to = lax.rem(self.me + d, self.n)
            self.go(send(self.got.at[place], self.got.at[place], self.s3.at[d], self.v3.at[d], to, self.rep))
            src = lax.rem(self.me + self.n - d, self.n)
            src_place = lax.rem(src, 2) * self.chips + lax.div(src, 2)
            self.c3.append(send(self.got.at[src_place], self.got.at[src_place],
                                self.s3.at[d], self.v3.at[d], to, self.rep))

    def finish(self):
        for copy in self.c3:
            copy.wait_recv()
        return self.got[...].reshape(self.n * self.ch, LANES)

    def drain(self):
        for copy in self.sends:
            copy.wait_send()


def put_grad(full, offset, grad, n_rep):
    share = grad.shape[0] // n_rep
    panels = grad.shape[1] // LANES
    low = grad.astype(BF16)
    for j in range(panels):
        full[:, offset + j * share : offset + (j + 1) * share, :] = low[
            :, j * LANES : (j + 1) * LANES
        ].reshape(n_rep, share, LANES)
    return offset + panels * share


def put_bias(full, offset, bias, n_rep):
    share = bias.shape[1] // n_rep
    count = full.shape[1] - offset
    first = lax.broadcasted_iota(jnp.int32, (count, LANES), 0) == 0
    for r in range(n_rep):
        row = bias[:, r * share : (r + 1) * share]
        if share < LANES:
            row = jnp.concatenate([row, jnp.zeros((1, LANES - share), F32)], axis=1)
        full[r, offset:, :] = jnp.where(first, row, 0.0).astype(BF16)


def take_grad(flat, offset, out, scale):
    share = out.shape[0]
    panels = out.shape[1] // LANES
    for j in range(panels):
        out[:, j * LANES : (j + 1) * LANES] = (
            flat[offset + j * share : offset + (j + 1) * share].astype(F32) * scale
        )
    return offset + panels * share


def take_bias(flat, offset, out, scale):
    rows = flat[offset : offset + 16].astype(F32) * scale
    out[...] = rows[0:1, : out.shape[1]]


def kernel(
    n_graph, n_rep,
    nodes, cot, live, partner, src_ref, dst_ref, we1, be, we2, wn1, bn, wn2,
    updated_out, dnodes_out, oe1, obe, oe2, on1, obn, on2,
    outgoing, arrived, keygrad, backsend, back, inv,
    x_send, x_recv, b_send, b_recv,
    *group_refs,
):
    me = lax.axis_index("graph")
    rep = lax.axis_index("rep")
    G, B, H = nodes.shape
    R = G * B
    half = G // 2
    E = src_ref.shape[1]
    per = len(group_refs) // 2
    node_group = Reduce(n_graph, n_rep, me, rep, group_refs[:per])
    edge_group = Reduce(n_graph, n_rep, me, rep, group_refs[per:])

    barrier = pltpu.get_barrier_semaphore()
    for d in range(1, n_graph):
        pl.semaphore_signal(barrier, inc=1, device_id={"graph": lax.rem(me + d, n_graph), "rep": rep},
                            device_id_type=pl.DeviceIdType.MESH)
    for d in range(1, n_rep):
        pl.semaphore_signal(barrier, inc=1, device_id={"graph": me, "rep": lax.rem(rep + d, n_rep)},
                            device_id_type=pl.DeviceIdType.MESH)

    def build(p, carry):
        lane = lax.broadcasted_iota(jnp.int32, (16, H), 1)
        row = lax.broadcasted_iota(jnp.int32, (16, H), 0)
        tile = jnp.zeros((16, H), F32)
        for h in range(2):
            first = jnp.int32(0)
            count = jnp.int32(0)
            for g in reversed(range(h * half, (h + 1) * half)):
                hit = partner[0, g] // G == p
                first = jnp.where(hit, g, first)
                count = count + jnp.where(hit, 1, 0)
            second = jnp.minimum(first + 1, G - 1)
            live1 = jnp.where(count > 0, live[0, first], 0)
            live2 = jnp.where(count > 1, live[0, second], 0)
            inv[0, p * 2 + h] = first
            inv[1, p * 2 + h] = count
            outgoing[p, h * GMAX * B : h * GMAX * B + B, :] = nodes[first]
            outgoing[p, h * GMAX * B + B : (h + 1) * GMAX * B, :] = nodes[second]
            bound = jnp.where(lane < B, live1, B + live2)
            bound = jnp.where(row == h, bound, 0)
            tile = tile + jnp.where(lane < bound, 1.0, 0.0)
        outgoing[p, 2 * GMAX * B :, :] = tile.astype(BF16)
        return carry

    lax.fori_loop(0, n_graph, build, 0)
    pl.semaphore_wait(barrier, n_graph + n_rep - 2)

    sends = []

    def exchange(src, dst, s_sem, r_sem):
        waits = []
        for d in range(1, n_graph):
            to = lax.rem(me + d, n_graph)
            frm = lax.rem(me + n_graph - d, n_graph)
            copy = send(src.at[to], dst.at[me], s_sem.at[d], r_sem.at[d], to, rep)
            copy.start()
            sends.append(copy)
            waits.append(send(src.at[to], dst.at[frm], s_sem.at[d], r_sem.at[d], to, rep))
        return waits

    waits = exchange(outgoing, arrived, x_send, x_recv)
    arrived[me] = outgoing[me]

    rows = nodes[...].reshape(R, H)
    row_ids = lax.broadcasted_iota(jnp.int32, (R, E), 0)
    hot = jnp.concatenate(
        [
            jnp.where(row_ids == dst_ref[...], 1.0, 0.0).astype(BF16),
            jnp.where(row_ids == src_ref[...], 1.0, 0.0).astype(BF16),
        ],
        axis=0,
    )
    pre = jnp.concatenate(
        [
            (dot_nn(rows, we1[:H]) + be[...]).astype(BF16),
            dot_nn(rows, we1[H:]).astype(BF16),
        ],
        axis=0,
    )
    summed = dot_tn(hot, pre)
    edge_sig = sigmoid(summed)
    gathered = dot_nn(hot[:R], (summed * edge_sig).astype(BF16)).astype(BF16)
    message = dot_nn(gathered, we2[...]).astype(BF16)
    hidden_pre = dot_nn(rows, wn1[:H]) + dot_nn(message, wn1[H : 2 * H]) + bn[...]
    position = lax.broadcasted_iota(jnp.int32, (B, H), 0)
    mask = jnp.concatenate(
        [jnp.where(position < live[0, g], 1.0, 0.0) for g in range(G)], axis=0
    ) > 0.5
    grad_out = jnp.where(mask, cot[...].reshape(R, H).astype(F32), 0.0).astype(BF16)
    back_hidden = dot_nt(grad_out, wn2[...])

    for copy in waits:
        copy.wait_recv()
    scale = H ** (-0.5)

    def peer(g):
        return partner[0, g] // G

    def keys_of(g):
        off = GMAX * B if g < half else 0
        return arrived[peer(g), off : off + GMAX * B, :]

    def block(values, g):
        return values[g * B : (g + 1) * B]

    score_list, mask_list = [], []
    for g in range(G):
        h = 1 if g < half else 0
        score_list.append(dot_nt(block(rows, g), keys_of(g)))
        tail = arrived[peer(g), 2 * GMAX * B :, :].astype(F32)
        mask_list.append(jnp.broadcast_to(tail[h : h + 1, : GMAX * B], (B, GMAX * B)))
    scores = jnp.concatenate(score_list, axis=0) * scale
    scores = jnp.where(jnp.concatenate(mask_list, axis=0) > 0.5, scores, -jnp.inf)
    powers = jnp.exp(scores - jnp.max(scores, axis=-1, keepdims=True))
    probs = powers / jnp.sum(powers, axis=-1, keepdims=True)
    low = probs.astype(BF16)
    context = jnp.concatenate([dot_nn(block(low, g), keys_of(g)) for g in range(G)], axis=0)
    moved = (rows.astype(F32) - context).astype(BF16)

    hidden_pre = hidden_pre + dot_nn(moved, wn1[2 * H :])
    sig = sigmoid(hidden_pre)
    active = (hidden_pre * sig).astype(BF16)
    grad_hidden = (back_hidden * silu_slope(hidden_pre, sig)).astype(BF16)
    grad_moved = dot_nt(grad_hidden, wn1[2 * H :]).astype(BF16)

    negated = -grad_moved
    grad_probs = jnp.concatenate(
        [dot_nt(block(negated, g), keys_of(g)) for g in range(G)], axis=0
    )
    inner = jnp.sum(probs * grad_probs, axis=-1, keepdims=True)
    grad_scores = (probs * (grad_probs - inner) * scale).astype(BF16)
    for g in range(G):
        left = jnp.concatenate([block(low, g), block(grad_scores, g)], axis=0)
        right = jnp.concatenate([block(negated, g), block(rows, g)], axis=0)
        keygrad[g] = dot_tn(left, right)

    def build_back(p, carry):
        for h in range(2):
            first = inv[0, p * 2 + h]
            count = inv[1, p * 2 + h]
            one = jnp.where(count > 0, 1.0, 0.0)
            two = jnp.where(count > 1, 1.0, 0.0)
            total = keygrad[first] * one + keygrad[jnp.minimum(first + 1, G - 1)] * two
            backsend[p, (1 - h) * GMAX : (2 - h) * GMAX] = total.astype(BF16).reshape(GMAX, B, H)
        return carry

    lax.fori_loop(0, n_graph, build_back, 0)
    back_waits = exchange(backsend, back, b_send, b_recv)
    back[me] = backsend[me]

    full = node_group.full
    pieces = jnp.concatenate(
        [dot_tn(rows, grad_hidden), dot_tn(message, grad_hidden), dot_tn(moved, grad_hidden)], axis=0
    )
    at = put_grad(full, 0, pieces, n_rep)
    at = put_grad(full, at, dot_tn(active, grad_out), n_rep)
    put_bias(full, at, jnp.sum(grad_hidden.astype(F32), axis=0, keepdims=True), n_rep)
    node_group.start_core()

    grad_message = dot_nt(grad_hidden, wn1[H : 2 * H]).astype(BF16)
    grad_gathered = dot_nt(grad_message, we2[...]).astype(BF16)
    edge_grad = (dot_tn(hot[:R], grad_gathered) * silu_slope(summed, edge_sig)).astype(BF16)
    both = dot_nn(hot, edge_grad).astype(BF16)
    grad_target, grad_source = both[:R], both[R:]
    node_group.start_plane()

    full = edge_group.full
    pieces = jnp.concatenate([dot_tn(rows, grad_target), dot_tn(rows, grad_source)], axis=0)
    at = put_grad(full, 0, pieces, n_rep)
    at = put_grad(full, at, dot_tn(gathered, grad_message), n_rep)
    put_bias(full, at, jnp.sum(grad_target.astype(F32), axis=0, keepdims=True), n_rep)
    edge_group.start_core()

    updated = jnp.where(mask, rows.astype(F32) + dot_nn(active, wn2[...]), 0.0)
    updated_out[...] = updated.astype(BF16).reshape(G, B, H)
    total = grad_out.astype(F32) + grad_moved.astype(F32)
    total = total + dot_nt(grad_hidden, wn1[:H])
    total = total + dot_nt(grad_target, we1[:H]) + dot_nt(grad_source, we1[H:])
    total = total + jnp.concatenate(
        [dot_nn(block(grad_scores, g), keys_of(g)) for g in range(G)], axis=0
    )
    edge_group.start_plane()
    for copy in back_waits:
        copy.wait_recv()
    returned = []
    for g in range(G):
        h = 0 if g < half else 1
        same = partner[0, g] == partner[0, g - 1] if g > 0 else False
        place = jnp.where(same, 1, 0)
        returned.append(back[peer(g), h * GMAX + place])
    total = total + jnp.concatenate(returned, axis=0).astype(F32)
    dnodes_out[...] = jnp.where(mask, total, 0.0).astype(BF16).reshape(G, B, H)

    node_group.start_rep()
    edge_group.start_rep()
    node_group.start_gather()
    edge_group.start_gather()
    grad_scale = (n_graph * n_rep * R) ** (-0.5)
    flat = node_group.finish()
    at = take_grad(flat, 0, on1, grad_scale)
    at = take_grad(flat, at, on2, grad_scale)
    take_bias(flat, at, obn, grad_scale)
    flat = edge_group.finish()
    at = take_grad(flat, 0, oe1, grad_scale)
    at = take_grad(flat, at, oe2, grad_scale)
    take_bias(flat, at, obe, grad_scale)
    for copy in sends:
        copy.wait_send()
    node_group.drain()
    edge_group.drain()


def group_scratch(shapes, n_graph, n_rep):
    rows = sum(s[0] // n_rep * (s[1] // LANES) for s in shapes)
    rows = round_up(rows + 16, 16 * n_graph)
    half, ch, chips = rows // 2, rows // n_graph, n_graph // 2
    dma = pltpu.SemaphoreType.DMA
    return [
        pltpu.VMEM((n_rep, rows, LANES), BF16),
        pltpu.VMEM((n_rep, half, LANES), BF16),
        pltpu.VMEM((n_rep, half, LANES), BF16),
        pltpu.VMEM((chips, n_rep, ch, LANES), BF16),
        pltpu.VMEM((n_rep, ch, LANES), BF16),
        pltpu.VMEM((n_rep, ch, LANES), BF16),
        pltpu.VMEM((n_graph, ch, LANES), BF16),
        dma((2,)),
        dma((chips,)),
        dma((chips,)),
        dma((n_rep,)),
        dma((n_rep,)),
        dma((n_graph,)),
        dma((n_graph,)),
    ]


def on_device(
    n_graph, n_rep,
    nodes, cotangent, live, partner_first, partner_size, edge_src, edge_dst,
    w_edge1, b_edge, w_edge2, w_node1, b_node, w_node2,
):
    _, G, B, H = nodes.shape
    FM = w_edge1.shape[1]
    rows_x = 2 * GMAX * B
    dma = pltpu.SemaphoreType.DMA
    vmem = pl.BlockSpec(memory_space=pltpu.VMEM)
    smem = pl.BlockSpec(memory_space=pltpu.SMEM)
    sds = jax.ShapeDtypeStruct

    def share(shape):
        return sds((shape[0] // n_rep,) + tuple(shape[1:]), F32)

    outs = pl.pallas_call(
        functools.partial(kernel, n_graph, n_rep),
        out_shape=(
            sds((G, B, H), BF16),
            sds((G, B, H), BF16),
            share(w_edge1.shape),
            sds((1, FM // n_rep), F32),
            share(w_edge2.shape),
            share(w_node1.shape),
            sds((1, FM // n_rep), F32),
            share(w_node2.shape),
        ),
        in_specs=[vmem, vmem, smem, smem] + [vmem] * 8,
        out_specs=(vmem,) * 8,
        scratch_shapes=[
            pltpu.VMEM((n_graph, rows_x + 16, H), BF16),
            pltpu.VMEM((n_graph, rows_x + 16, H), BF16),
            pltpu.VMEM((G, GMAX * B, H), F32),
            pltpu.VMEM((n_graph, 2 * GMAX, B, H), BF16),
            pltpu.VMEM((n_graph, 2 * GMAX, B, H), BF16),
            pltpu.SMEM((2, 2 * n_graph), jnp.int32),
            dma((n_graph,)),
            dma((n_graph,)),
            dma((n_graph,)),
            dma((n_graph,)),
        ]
        + group_scratch([w_node1.shape, w_node2.shape], n_graph, n_rep)
        + group_scratch([w_edge1.shape, w_edge2.shape], n_graph, n_rep),
        compiler_params=pltpu.CompilerParams(
            collective_id=0, has_side_effects=True, vmem_limit_bytes=64 * 1000 * 1000
        ),
    )(
        nodes[0], cotangent[0], live, partner_first, edge_src, edge_dst,
        w_edge1, b_edge.reshape(1, FM), w_edge2, w_node1, b_node.reshape(1, FM), w_node2,
    )
    return (
        outs[0][None],
        outs[1][None],
        outs[2],
        outs[3].reshape(-1),
        outs[4],
        outs[5],
        outs[6].reshape(-1),
        outs[7],
    )


def solution(mesh):
    rows = P("rep", "graph", None, None)
    ints = P("rep", "graph")
    return jax.shard_map(
        functools.partial(on_device, mesh.shape["graph"], mesh.shape["rep"]),
        mesh=mesh,
        in_specs=(rows, rows, ints, ints, ints, ints, ints) + (P(),) * 6,
        out_specs=(
            rows,
            rows,
            P("rep", None),
            P("rep"),
            P("rep", None),
            P("rep", None),
            P("rep"),
            P("rep", None),
        ),
        check_vma=False,
    )
```

time: 224 us -> 52.6 us (0.23)
  waiting for transfers between devices: 83.1 us -> 0 us
  blocking collectives: 46.2 us -> 0 us
  Pallas kernels: 0 us -> 45.7 us
  other arithmetic: 26.5 us -> 0 us
  matrix products: 25 us -> 0 us
  between operations: 14.6 us -> 0.67 us
  starting transfers between devices: 13.1 us -> 0 us
  local copies, waits for them, and re-layouts: 14.6 us -> 6.08 us
    psum x1 -> x0, waiting for transfers between devices: 75.9 us -> none  [on_device(): lax.psum((partial_grads[0], partial_grads[1], partial_grads[2], partial_g...]
    psum x1 -> x0, blocking collectives: 46.2 us -> none  [on_device(): lax.psum((partial_grads[0], partial_grads[1], partial_grads[2], partial_g...]
    pallas_call x0 -> x1, Pallas kernels: none -> 45.7 us  [on_device(): pl.pallas_call(functools.partial(kernel, n_graph, n_rep), out_shape=(sds(...]
    dot_general x27 -> x0, matrix products: 25 us -> none  [the longest x1 2.33 us: attend_back(): jnp.einsum('gqk,gqh->gkh', grad_scores, queries, preferred_element_type=j...]
    all_to_all x3 -> x0, starting transfers between devices: 13 us -> none  [the longest x1 5.2 us: on_device(): lax.all_to_all(lives_out, 'graph', split_axis=0, concat_axis=0, tiled=True)]
    scatter-add x4 -> x0, other arithmetic: 9.05 us -> none  [the longest x1 2.76 us: message_backward(): jax.ops.segment_sum(edge_grad, sources, num_segments=node_rows.shape[0])]
    mul x6 -> x0, other arithmetic: 7.76 us -> none  [on_device(): scaled = tuple((summed_grad * scale_factor for summed_grad in shares))]
    gather x7 -> x0, local copies, waits for them, and re-layouts: 7.58 us -> none  [the longest x1 1.79 us: on_device(): attention_grad = query_all + back_grad[send_slot]]
  transfers between devices with their start and end apart: 4 -> 0, of which waited for: 2 -> 0; matrix products, arithmetic and copies ran while one was open for 14% -> 0% of each run, Pallas kernels for 0% -> 0%
where the time goes in v1:
time: 52.6 us; the launch traced here: 52.5 us
  Pallas kernels  45.7 us (87%)
  local copies, waits for them, and re-layouts  6.08 us (12%)
  between operations  0.67 us (1%)
    pallas_call x1, Pallas kernels, on_device(): pl.pallas_call(functools.partial(kernel, n_graph, n_rep), out_shape=(sds(...  45.7 us
    unnamed x22, local copies, waits for them, and re-layouts  6.08 us

profile of v1, /device:TPU:0, one launch (start us, length us, event | category | flops | bytes accessed | tf_op | source)
XLA Modules:
  0.0 52.5 jit_solution(12146917870135407588)
XLA Ops:
  0.6 45.7 %shard_map.179 = (bf16[8,32,256]{2,1,0:T(8,128)(2,1)}, bf16[8,32,256]{2,1,0:T(8,128)(2,1)}, f32[128,512]{1,0:T(8,128)}, f32[1,128]{1,0:T(1,128)}, f32[128,256]{1...) custom-call(bf16[8,32,256]{2,1,0:T(8,128)(2,1)} %bitcast.8, bf16[8,32,256]{2,1,0:T(8,128)(2,1)} %bitcast.9, ...), custom_call_target="tpu_custom_call" | custom-call | tf_op jit(solution)/shard_map/pallas_call | solution.py:423
  46.3 0.0 copy-start.4
  46.4 0.0 copy-start.1
  46.4 1.6 %copy.28 = bf16[1,8,32,256]{3,2,1,0:T(8,128)(2,1)} copy(bf16[1,8,32,256]{3,2,1,0:T(8,128)(2,1)} %bitcast.11) | data formatting | bytes 262144
  48.0 0.0 copy-done.4
  48.0 0.0 copy-start.6
  48.0 0.7 %copy.29 = bf16[1,8,32,256]{3,2,1,0:T(8,128)(2,1)} copy(bf16[1,8,32,256]{3,2,1,0:T(8,128)(2,1)S(1)} %bitcast.10) | data formatting | bytes 262144
  48.6 0.0 copy-done.1
  48.6 0.0 copy-start.3
  48.6 0.0 copy-start
  48.7 0.7 %copy.30 = f32[128,512]{1,0:T(8,128)} copy(f32[128,512]{1,0:T(8,128)S(1)} %copy-done.1) | data formatting | bytes 524288
  49.4 0.0 copy-done.6
  49.4 0.5 copy.31
  49.9 0.0 copy-done.3
  49.9 0.7 %copy.32 = f32[128,256]{1,0:T(8,128)} copy(f32[128,256]{1,0:T(8,128)S(1)} %copy-done.3) | data formatting | bytes 262144
  50.5 0.0 copy-done
  50.5 0.0 copy-start.5
  50.5 0.0 copy-start.2
  50.5 0.7 %copy.33 = f32[192,512]{1,0:T(8,128)} copy(f32[192,512]{1,0:T(8,128)S(1)} %copy-done) | data formatting | bytes 786432
  51.3 0.0 copy-done.5
  51.3 0.5 copy.34
  51.8 0.0 copy-done.2
  51.8 0.7 %copy.35 = f32[128,256]{1,0:T(8,128)} copy(f32[128,256]{1,0:T(8,128)S(1)} %copy-done.2) | data formatting | bytes 262144
Async XLA Ops:
  46.3 1.6 %copy-start.4 = (bf16[8,32,256]{2,1,0:T(8,128)(2,1)S(1)}, bf16[8,32,256]{2,1,0:T(8,128)(2,1)}, u32[]{:S(2)}) copy-start(bf16[8,32,256]{2,1,0:T(8,128)(2,1)} %get-tuple-element.17) | copy-start | bytes 393220
  46.4 2.3 %copy-start.1 = (f32[128,512]{1,0:T(8,128)S(1)}, f32[128,512]{1,0:T(8,128)}, u32[]{:S(2)}) copy-start(f32[128,512]{1,0:T(8,128)} %get-tuple-element.34) | copy-start | bytes 786436
  48.0 1.4 %copy-start.6 = (f32[1,128]{1,0:T(1,128)S(1)}, f32[1,128]{1,0:T(1,128)}, u32[]{:S(2)}) copy-start(f32[1,128]{1,0:T(1,128)} %get-tuple-element.19) | copy-start | bytes 1540
  48.6 1.2 %copy-start.3 = (f32[128,256]{1,0:T(8,128)S(1)}, f32[128,256]{1,0:T(8,128)}, u32[]{:S(2)}) copy-start(f32[128,256]{1,0:T(8,128)} %get-tuple-element.36) | copy-start | bytes 393220
  48.6 1.9 %copy-start = (f32[192,512]{1,0:T(8,128)S(1)}, f32[192,512]{1,0:T(8,128)}, u32[]{:S(2)}) copy-start(f32[192,512]{1,0:T(8,128)} %get-tuple-element.37) | copy-start | bytes 1179652
  50.5 0.8 %copy-start.5 = (f32[1,128]{1,0:T(1,128)S(1)}, f32[1,128]{1,0:T(1,128)}, u32[]{:S(2)}) copy-start(f32[1,128]{1,0:T(1,128)} %get-tuple-element.22) | copy-start | bytes 1540
  50.5 1.3 %copy-start.2 = (f32[128,256]{1,0:T(8,128)S(1)}, f32[128,256]{1,0:T(8,128)}, u32[]{:S(2)}) copy-start(f32[128,256]{1,0:T(8,128)} %get-tuple-element.39) | copy-start | bytes 393220
